TPU v7x, 32 devices: a whole 2x2x4 slice. The times are simulated.
32 devices in a mesh: row: 4 (over y, core), col: 8 (over z, x).
Axes of the slice: x: 2, y: 2, z: 4, core: 2. Of those that a mesh axis runs over, the one named last changes fastest.
Arguments:
- tokens: bfloat16 [512, 8192], P('col', 'row'), may hold values from -6 to 6
- norm_gain: float32 [8192], P('row'), may hold values from 0.1 to 1.9
- gate_weight: bfloat16 [8192, 28672], P('row', 'col'), may hold values from -0.0625 to 0.0625
- up_weight: bfloat16 [8192, 28672], P('row', 'col'), may hold values from -0.0625 to 0.0625
- down_weight: bfloat16 [28672, 8192], P('col', 'row'), may hold values from -0.03125 to 0.03125
Outputs:
- block_out: bfloat16 [512, 8192], P('col', 'row')
All inputs are finite; a program needn't handle non-finite values.
Results may differ from a plain program's by a relative error of at most 0.0017.
Values may be sent and summed in bfloat16 or wider, within the bound.
A program may use at most 128 MiB of HBM per device.

v0:
```python
import jax
import jax.numpy as jnp
from jax import lax
from jax.sharding import PartitionSpec as P

D = 8192
epsilon = 1e-05


def local(tokens, norm_gain, gate_weight, up_weight, down_weight):
    gain_row = norm_gain.astype(jnp.float32)[None, :]
    gathered = lax.all_gather(tokens, "col", axis=0, tiled=True)
    values = gathered.astype(jnp.float32)
    squares = lax.psum(jnp.sum(values * values, axis=1), "row")
    normed = (values * lax.rsqrt(squares[:, None] / D + epsilon) * gain_row).astype(jnp.bfloat16)
    gate_part = jnp.dot(normed, gate_weight, preferred_element_type=jnp.float32)
    up_part = jnp.dot(normed, up_weight, preferred_element_type=jnp.float32)
    gate_sum, up_sum = (
        lax.psum_scatter(gate_part, "row", scatter_dimension=0, tiled=True),
        lax.psum_scatter(up_part, "row", scatter_dimension=0, tiled=True),
    )
    local_hidden = (jax.nn.silu(gate_sum) * up_sum).astype(jnp.bfloat16)
    hidden = lax.all_gather(local_hidden, "row", axis=0, tiled=True)

    def down_term(length):
        row_block = lax.slice_in_dim(hidden, 0, length, axis=0)
        return jnp.dot(row_block, down_weight, preferred_element_type=jnp.float32)

    branch_out = lax.psum_scatter(
        down_term(lax.axis_size("col") * tokens.shape[0]), "col", scatter_dimension=0, tiled=True
    )
    return (tokens.astype(jnp.float32) + branch_out).astype(jnp.bfloat16)


def solution(mesh):
    placed = (P("col", "row"), P("row"), P("row", "col"), P("row", "col"), P("col", "row"))
    return jax.shard_map(
        local, mesh=mesh, in_specs=placed, out_specs=P("col", "row"), check_vma=False
    )
```

profile of v0, /device:TPU:0, one launch (start us, length us, event | category | flops | bytes accessed | tf_op | source)
XLA Modules:
  0.0 361.5 jit_solution(13591276353215433253)
XLA Ops:
  6.5 0.0 all-gather.3.cloned.1.call-start
  6.5 0.7 all-gather.3.cloned.1.call-update
  7.3 0.0 reduce-scatter.6.cloned.1.call-start
  7.3 54.0 %all-gather.3.cloned.1.call-done = bf16[512,2048]{1,0:T(8,128)(2,1)} async-done(((bf16[64,2048]{1,0:T(8,128)(2,1)}), bf16[512,2048]{1,0:T(8,128)(2,1)}) %all-gather.3.cloned.1.call-update) | async-done | bytes 2097168 | tf_op jit(solution)/shard_map/all_gather | solution.py:12
  61.3 2.1 fusion
  63.4 5.7 %psum.7 = f32[512]{0:T(512)S(1)} all-reduce(f32[512]{0:T(512)S(1)} %fusion), channel_id=1, replica_groups=mesh['row'=4,'col'=8] {'row'}, use_global_device_ids=true, to_apply=%region_1.0 | all-reduce | flops 512 | bytes 4096 | tf_op jit(solution)/shard_map/psum | solution.py:14
  69.0 13.6 %fusion.3 = f32[512,3584]{1,0:T(8,128)} fusion(bf16[2048,3584]{1,0:T(8,128)(2,1)} %param.8, bf16[512,2048]{1,0:T(8,128)(2,1)} %all-gather.3.cloned.1.call-done, f32[2048]{0:T(1024)} %param.6, f32[512]{0:T(512)S(1)} %add_rsqrt_fusion), kind=kOutput, calls=%fused_computation.6 | convolution fusion | flops 7520387072 | bytes 24127488 | tf_op jit(solution)/shard_map/dot_general | solution.py:17
  82.7 0.0 copy-start
  82.7 0.0 copy-start.2
  82.7 0.0 reduce-scatter.6.cloned.1.call-update
  82.7 0.0 reduce-scatter.4.cloned.1.call-start
  82.7 1.5 copy-done
  84.3 0.0 copy-done.2
  84.3 13.4 %fusion.5 = f32[512,3584]{1,0:T(8,128)} fusion(bf16[2048,3584]{1,0:T(8,128)(2,1)} %param.7, bf16[512,2048]{1,0:T(8,128)(2,1)S(1)} %copy-done, f32[2048]{0:T(1024)S(1)} %copy-done.2, f32[512]{0:T(512)S(1)} %add_rsqrt_fusion), kind=kOutput, calls=%fused_computation.7 | convolution fusion | flops 7520387072 | bytes 24127488 | tf_op jit(solution)/shard_map/dot_general | solution.py:16
  97.7 0.0 reduce-scatter.4.cloned.1.call-update
  97.7 0.0 all-gather.5.cloned.1.call-start
  97.8 49.8 %reduce-scatter.6.cloned.1.call-done = f32[128,3584]{1,0:T(8,128)} async-done(((f32[512,3584]{1,0:T(8,128)}), f32[128,3584]{1,0:T(8,128)}) %reduce-scatter.6.cloned.1.call-update) | async-done | bytes 1835024 | tf_op jit(solution)/shard_map/reduce_scatter | solution.py:20
  147.6 68.5 %reduce-scatter.4.cloned.1.call-done = f32[128,3584]{1,0:T(8,128)} async-done(((f32[512,3584]{1,0:T(8,128)}), f32[128,3584]{1,0:T(8,128)}) %reduce-scatter.4.cloned.1.call-update) | async-done | bytes 1835024 | tf_op jit(solution)/shard_map/reduce_scatter | solution.py:19
  216.1 3.5 multiply_convert_fusion
  219.6 0.0 all-gather.5.cloned.1.call-update
  219.6 0.0 reduce-scatter.8.cloned.1.call-start
  219.7 31.6 %all-gather.5.cloned.1.call-done = bf16[512,3584]{1,0:T(8,128)(2,1)} async-done(((bf16[128,3584]{1,0:T(8,128)(2,1)}), bf16[512,3584]{1,0:T(8,128)(2,1)}) %all-gather.5.cloned.1.call-update) | async-done | bytes 3670032 | tf_op jit(solution)/shard_map/all_gather | solution.py:23
  251.3 13.4 %fusion.7 = f32[512,2048]{1,0:T(8,128)} fusion(bf16[512,3584]{1,0:T(8,128)(2,1)} %all-gather.5.cloned.1.call-done, bf16[3584,2048]{1,0:T(8,128)(2,1)} %param.9), kind=kOutput, calls=%fused_computation.10 | convolution fusion | flops 7516192768 | bytes 22544384 | tf_op jit(solution)/shard_map/dot_general | solution.py:27
  264.7 0.0 copy-start.1
  264.7 0.0 reduce-scatter.8.cloned.1.call-update
  264.7 88.5 %reduce-scatter.8.cloned.1.call-done = f32[64,2048]{1,0:T(8,128)} async-done(((f32[512,2048]{1,0:T(8,128)}), f32[64,2048]{1,0:T(8,128)}) %reduce-scatter.8.cloned.1.call-update) | async-done | bytes 524304 | tf_op jit(solution)/shard_map/reduce_scatter | solution.py:29
  353.2 0.0 copy-done.1
  353.2 1.8 add_convert_fusion
  (1 shorter events, 0.0 us)
Async XLA Ops:
  6.5 54.8 %all-gather.3.cloned.1.call-start = ((), (), s32[]{:S(2)}) async-start(), calls=%async_computation.3 | async-start | bytes 2359296 | tf_op jit(solution)/shard_map/all_gather | solution.py:12
  7.3 140.3 %reduce-scatter.6.cloned.1.call-start = ((), (), s32[]{:S(2)}) async-start(), calls=%async_computation.5 | async-start | bytes 9175040 | tf_op jit(solution)/shard_map/reduce_scatter | solution.py:20
  82.7 1.6 copy-start
  82.7 1.6 copy-start.2
  82.7 133.4 %reduce-scatter.4.cloned.1.call-start = ((), (), s32[]{:S(2)}) async-start(), calls=%async_computation.4 | async-start | bytes 9175040 | tf_op jit(solution)/shard_map/reduce_scatter | solution.py:19
  97.7 153.6 %all-gather.5.cloned.1.call-start = ((), (), s32[]{:S(2)}) async-start(), calls=%async_computation.6 | async-start | bytes 4587520 | tf_op jit(solution)/shard_map/all_gather | solution.py:23
  219.6 133.5 %reduce-scatter.8.cloned.1.call-start = ((), (), s32[]{:S(2)}) async-start(), calls=%async_computation.7 | async-start | bytes 4718592 | tf_op jit(solution)/shard_map/reduce_scatter | solution.py:29
  264.7 88.5 %copy-start.1 = (bf16[64,2048]{1,0:T(8,128)(2,1)S(1)}, bf16[64,2048]{1,0:T(8,128)(2,1)}, u32[]{:S(2)}) copy-start(bf16[64,2048]{1,0:T(8,128)(2,1)} %param.5) | copy-start | bytes 786436
Sparse Core Ops, SparseCore 0:
  9.5 51.7 all-gather.2
  82.8 64.7 reduce-scatter.5
  150.1 65.9 reduce-scatter.3
  219.8 31.4 all-gather.4
  264.8 88.2 reduce-scatter.7
where the time goes:
time: 362 us; the launch traced here: 361 us
  waiting for transfers between devices  293 us (81%)
  matrix products  40.5 us (11%)
  between operations  13.1 us (4%)
  other arithmetic  7.36 us (2%)
  blocking collectives  5.66 us (2%)
    reduce_scatter x1, waiting for transfers between devices, local(): lax.psum_scatter(down_term(lax.axis_size('col') * tokens.shape[0]), 'col'...  88.5 us
    reduce_scatter x1, waiting for transfers between devices, local(): lax.psum_scatter(gate_part, 'row', scatter_dimension=0, tiled=True)  68.5 us
    all_gather x1, waiting for transfers between devices, local(): gathered = lax.all_gather(tokens, 'col', axis=0, tiled=True)  54 us
    reduce_scatter x1, waiting for transfers between devices, local(): lax.psum_scatter(up_part, 'row', scatter_dimension=0, tiled=True)  49.8 us
    all_gather x1, waiting for transfers between devices, local(): hidden = lax.all_gather(local_hidden, 'row', axis=0, tiled=True)  31.6 us
    dot_general x1, matrix products, local(): up_part = jnp.dot(normed, up_weight, preferred_element_type=jnp.float32)  13.6 us
    dot_general x1, matrix products, local(): gate_part = jnp.dot(normed, gate_weight, preferred_element_type=jnp.float32)  13.4 us
    dot_general x1, matrix products, down_term(): return jnp.dot(row_block, down_weight, preferred_element_type=jnp.float32)  13.4 us
  transfers between devices with their start and end apart: 5, of which 5 were waited for; matrix products, arithmetic and copies ran while one was open for 4% of the time, Pallas kernels for 0%

commit v1 on v0

--- a/solution.py
+++ b/solution.py
@@ -9,7 +9,13 @@
 
 def local(tokens, norm_gain, gate_weight, up_weight, down_weight):
     gain_row = norm_gain.astype(jnp.float32)[None, :]
-    gathered = lax.all_gather(tokens, "col", axis=0, tiled=True)
+    gathered = lax.all_to_all(
+        jnp.concatenate([tokens for _ in range(lax.axis_size("col"))], axis=0),
+        "col",
+        0,
+        0,
+        tiled=True,
+    )
     values = gathered.astype(jnp.float32)
     squares = lax.psum(jnp.sum(values * values, axis=1), "row")
     normed = (values * lax.rsqrt(squares[:, None] / D + epsilon) * gain_row).astype(jnp.bfloat16)

time: 362 us -> 367 us (1.014)
  blocking collectives: 5.66 us -> 60.9 us
  waiting for transfers between devices: 293 us -> 239 us
  local copies, waits for them, and re-layouts: 1.52 us -> 7 us
    all_to_all x0 -> x1, blocking collectives: none -> 55.3 us  [local(): lax.all_to_all(jnp.concatenate([tokens for _ in range(lax.axis_size('col'...]
    all_gather x1 -> x0, waiting for transfers between devices: 54 us -> none  [local(): gathered = lax.all_gather(tokens, 'col', axis=0, tiled=True)]
    unnamed x6 -> x15, local copies, waits for them, and re-layouts: 1.52 us -> 6.9 us
  transfers between devices with their start and end apart: 5 -> 4, of which waited for: 5 -> 4; matrix products, arithmetic and copies ran while one was open for 4% -> 4% of each run, Pallas kernels for 0% -> 0%
where the time goes in v1:
time: 367 us; the launch traced here: 366 us
  waiting for transfers between devices  239 us (65%)
  blocking collectives  60.9 us (17%)
  matrix products  39.2 us (11%)
  between operations  13.2 us (4%)
  local copies, waits for them, and re-layouts  7 us (2%)
  other arithmetic  6.3 us (2%)
    reduce_scatter x1, waiting for transfers between devices, local(): lax.psum_scatter(down_term(lax.axis_size('col') * tokens.shape[0]), 'col'...  88.5 us
    reduce_scatter x1, waiting for transfers between devices, local(): lax.psum_scatter(gate_part, 'row', scatter_dimension=0, tiled=True)  68.5 us
    all_to_all x1, blocking collectives, local(): lax.all_to_all(jnp.concatenate([tokens for _ in range(lax.axis_size('col'...  55.3 us
    reduce_scatter x1, waiting for transfers between devices, local(): lax.psum_scatter(up_part, 'row', scatter_dimension=0, tiled=True)  50.8 us
    all_gather x1, waiting for transfers between devices, local(): hidden = lax.all_gather(local_hidden, 'row', axis=0, tiled=True)  31.6 us
    dot_general x1, matrix products, down_term(): return jnp.dot(row_block, down_weight, preferred_element_type=jnp.float32)  13.4 us
    dot_general x1, matrix products, local(): gate_part = jnp.dot(normed, gate_weight, preferred_element_type=jnp.float32)  12.9 us
    dot_general x1, matrix products, local(): up_part = jnp.dot(normed, up_weight, preferred_element_type=jnp.float32)  12.9 us
  transfers between devices with their start and end apart: 4, of which 4 were waited for; matrix products, arithmetic and copies ran while one was open for 4% of the time, Pallas kernels for 0%

profile of v1, /device:TPU:0, one launch (start us, length us, event | category | flops | bytes accessed | tf_op | source)
XLA Modules:
  0.0 366.2 jit_solution(1695974234622388195)
XLA Ops:
  6.5 0.0 copy-start
  6.5 0.0 reduce-scatter.6.cloned.1.call-start
  6.5 1.0 constant_dynamic-update-slice_fusion.7
  7.6 1.0 constant_dynamic-update-slice_fusion.6
  8.6 1.0 constant_dynamic-update-slice_fusion.5
  9.5 1.0 constant_dynamic-update-slice_fusion.4
  10.5 0.0 copy-done
  10.6 55.3 %all_to_all.9 = bf16[8,64,2048]{2,1,0:T(8,128)(2,1)S(1)} all-to-all(bf16[8,64,2048]{2,1,0:T(8,128)(2,1)S(1)} %bitcast.13), channel_id=1, replica_groups=mesh['row'=4,'col'=8] {'col'}, dimensions={0} | all-to-all | bytes 4194304 | tf_op jit(solution)/shard_map/all_to_all | solution.py:12
  65.9 0.0 copy-start.3
  65.9 0.5 multiply_reduce_fusion
  66.4 0.1 reduce_sum.12
  66.5 5.6 %psum.7 = f32[512]{0:T(512)S(1)} all-reduce(f32[512]{0:T(512)S(1)} %reduce_sum.12), channel_id=1, replica_groups=mesh['row'=4,'col'=8] {'row'}, use_global_device_ids=true, to_apply=%region_1.0 | all-reduce | flops 512 | bytes 4096 | tf_op jit(solution)/shard_map/psum | solution.py:20
  72.1 0.0 copy-done.3
  72.1 0.5 fusion.1
  72.7 0.0 copy-start.1
  72.7 1.4 copy-done.1
  74.1 12.9 %fusion.3 = f32[512,3584]{1,0:T(8,128)} fusion(bf16[512,2048]{1,0:T(8,128)(2,1)S(1)} %fusion.1, bf16[2048,3584]{1,0:T(8,128)(2,1)} %param.8), kind=kOutput, calls=%fused_computation.16 | convolution fusion | flops 7516192768 | bytes 24117248 | tf_op jit(solution)/shard_map/dot_general | solution.py:23
  87.0 0.0 copy-start.2
  87.0 0.0 reduce-scatter.6.cloned.1.call-update
  87.0 0.0 reduce-scatter.4.cloned.1.call-start
  87.0 1.5 copy-done.2
  88.6 12.9 %fusion.2 = f32[512,3584]{1,0:T(8,128)} fusion(bf16[512,2048]{1,0:T(8,128)(2,1)S(1)} %copy-done.2, bf16[2048,3584]{1,0:T(8,128)(2,1)} %param.7), kind=kOutput, calls=%fused_computation.15 | convolution fusion | flops 7516192768 | bytes 24117248 | tf_op jit(solution)/shard_map/dot_general | solution.py:22
  101.5 0.0 reduce-scatter.4.cloned.1.call-update
  101.5 0.0 all-gather.2.cloned.1.call-start
  101.5 50.8 %reduce-scatter.6.cloned.1.call-done = f32[128,3584]{1,0:T(8,128)} async-done(((f32[512,3584]{1,0:T(8,128)}), f32[128,3584]{1,0:T(8,128)}) %reduce-scatter.6.cloned.1.call-update) | async-done | bytes 1835024 | tf_op jit(solution)/shard_map/reduce_scatter | solution.py:26
  152.3 68.5 %reduce-scatter.4.cloned.1.call-done = f32[128,3584]{1,0:T(8,128)} async-done(((f32[512,3584]{1,0:T(8,128)}), f32[128,3584]{1,0:T(8,128)}) %reduce-scatter.4.cloned.1.call-update) | async-done | bytes 1835024 | tf_op jit(solution)/shard_map/reduce_scatter | solution.py:25
  220.8 3.5 multiply_convert_fusion
  224.3 0.0 all-gather.2.cloned.1.call-update
  224.3 0.0 reduce-scatter.8.cloned.1.call-start
  224.4 31.6 %all-gather.2.cloned.1.call-done = bf16[512,3584]{1,0:T(8,128)(2,1)} async-done(((bf16[128,3584]{1,0:T(8,128)(2,1)}), bf16[512,3584]{1,0:T(8,128)(2,1)}) %all-gather.2.cloned.1.call-update) | async-done | bytes 3670032 | tf_op jit(solution)/shard_map/all_gather | solution.py:29
  256.0 13.4 %fusion.4 = f32[512,2048]{1,0:T(8,128)} fusion(bf16[512,3584]{1,0:T(8,128)(2,1)} %all-gather.2.cloned.1.call-done, bf16[3584,2048]{1,0:T(8,128)(2,1)} %param.9), kind=kOutput, calls=%fused_computation.17 | convolution fusion | flops 7516192768 | bytes 22544384 | tf_op jit(solution)/shard_map/dot_general | solution.py:33
  269.4 0.0 reduce-scatter.8.cloned.1.call-update
  269.4 88.5 %reduce-scatter.8.cloned.1.call-done = f32[64,2048]{1,0:T(8,128)} async-done(((f32[512,2048]{1,0:T(8,128)}), f32[64,2048]{1,0:T(8,128)}) %reduce-scatter.8.cloned.1.call-update) | async-done | bytes 524304 | tf_op jit(solution)/shard_map/reduce_scatter | solution.py:35
  357.8 1.8 add_convert_fusion
  (5 shorter events, 0.1 us)
Async XLA Ops:
  6.5 4.0 %copy-start = (bf16[64,2048]{1,0:T(8,128)(2,1)S(1)}, bf16[64,2048]{1,0:T(8,128)(2,1)}, u32[]{:S(2)}) copy-start(bf16[64,2048]{1,0:T(8,128)(2,1)} %param.5) | copy-start | bytes 786436
  6.5 145.8 %reduce-scatter.6.cloned.1.call-start = ((), (), s32[]{:S(2)}) async-start(), calls=%async_computation.5 | async-start | bytes 9175040 | tf_op jit(solution)/shard_map/reduce_scatter | solution.py:26
  65.9 6.2 %copy-start.3 = (f32[2048]{0:T(1024)S(1)}, f32[2048]{0:T(1024)}, u32[]{:S(2)}) copy-start(f32[2048]{0:T(1024)} %param.6) | copy-start | bytes 24580
  72.7 1.4 copy-start.1
  87.0 1.6 copy-start.2
  87.0 133.9 %reduce-scatter.4.cloned.1.call-start = ((), (), s32[]{:S(2)}) async-start(), calls=%async_computation.4 | async-start | bytes 9175040 | tf_op jit(solution)/shard_map/reduce_scatter | solution.py:25
  101.5 154.5 %all-gather.2.cloned.1.call-start = ((), (), s32[]{:S(2)}) async-start(), calls=%async_computation.6 | async-start | bytes 4587520 | tf_op jit(solution)/shard_map/all_gather | solution.py:29
  224.3 133.5 %reduce-scatter.8.cloned.1.call-start = ((), (), s32[]{:S(2)}) async-start(), calls=%async_computation.7 | async-start | bytes 4718592 | tf_op jit(solution)/shard_map/reduce_scatter | solution.py:35
Sparse Core Ops, SparseCore 0:
  87.1 65.1 reduce-scatter.5
  154.9 65.9 reduce-scatter.3
  224.5 31.4 all-gather.1
  269.5 88.2 reduce-scatter.7

commit v2 on v0

--- a/solution.py
+++ b/solution.py
@@ -2,9 +2,31 @@
 import jax.numpy as jnp
 from jax import lax
 from jax.sharding import PartitionSpec as P
+from jax.lax import axis_index, axis_size, ppermute
 
 D = 8192
 epsilon = 1e-05
+
+
+def fill_keys_here(x0, array_axis):
+    x0 = jnp.moveaxis(x0, 0, array_axis)
+    v_next = x0.shape
+    x_now = x0.reshape(
+        *v_next[:array_axis], v_next[array_axis] * v_next[array_axis + 1], *v_next[array_axis + 2 :]
+    )
+    return x_now
+
+
+def bring_ends(sheet, along_axis):
+    num = axis_size(along_axis)
+    block_now = sheet[None]
+    for q in range(num.bit_length() - 1):
+        before = 1 << q
+        piece_out = ppermute(block_now, along_axis, [(i0, i0 ^ before) for i0 in range(num)])
+        met_up = jnp.stack([block_now, piece_out])
+        current_value = axis_index(along_axis) >> q & 1
+        block_now = jnp.where(current_value == 0, met_up, met_up[::-1]).reshape(-1, *sheet.shape)
+    return block_now
 
 
 def local(tokens, norm_gain, gate_weight, up_weight, down_weight):
@@ -20,7 +42,8 @@
         lax.psum_scatter(up_part, "row", scatter_dimension=0, tiled=True),
     )
     local_hidden = (jax.nn.silu(gate_sum) * up_sum).astype(jnp.bfloat16)
-    hidden = lax.all_gather(local_hidden, "row", axis=0, tiled=True)
+    r_now = bring_ends(local_hidden, "row")
+    hidden = fill_keys_here(r_now, 0)
 
     def down_term(length):
         row_block = lax.slice_in_dim(hidden, 0, length, axis=0)

time: 362 us -> 377 us (1.041)
  waiting for transfers between devices: 293 us -> 307 us
  other arithmetic: 7.36 us -> 11.5 us
    ppermute x0 -> x2, waiting for transfers between devices: none -> 44 us  [bring_ends(): ppermute(block_now, along_axis, [(i0, i0 ^ before) for i0 in range(num)])]
    all_gather x1 -> x0, waiting for transfers between devices: 31.6 us -> none  [local(): hidden = lax.all_gather(local_hidden, 'row', axis=0, tiled=True)]
    reduce_scatter x1, waiting for transfers between devices: 49.8 us -> 68.5 us  [local(): lax.psum_scatter(up_part, 'row', scatter_dimension=0, tiled=True)]
    reduce_scatter x1, waiting for transfers between devices: 68.5 us -> 51.8 us  [local(): lax.psum_scatter(gate_part, 'row', scatter_dimension=0, tiled=True)]
    another operation x0 -> x4, other arithmetic: none -> 4.13 us  [bring_ends(): met_up = jnp.stack([block_now, piece_out])]
  transfers between devices with their start and end apart: 5 -> 6, of which waited for: 5 -> 6; matrix products, arithmetic and copies ran while one was open for 4% -> 4% of each run, Pallas kernels for 0% -> 0%
where the time goes in v2:
time: 377 us
  waiting for transfers between devices  307 us (81%)
  matrix products  38.4 us (10%)
  between operations  13.2 us (4%)
  other arithmetic  11.5 us (3%)
  blocking collectives  5.66 us (2%)
    reduce_scatter x1, waiting for transfers between devices, local(): lax.psum_scatter(down_term(lax.axis_size('col') * tokens.shape[0]), 'col'...  88.4 us
    reduce_scatter x1, waiting for transfers between devices, local(): lax.psum_scatter(up_part, 'row', scatter_dimension=0, tiled=True)  68.5 us
    all_gather x1, waiting for transfers between devices, local(): gathered = lax.all_gather(tokens, 'col', axis=0, tiled=True)  54 us
    reduce_scatter x1, waiting for transfers between devices, local(): lax.psum_scatter(gate_part, 'row', scatter_dimension=0, tiled=True)  51.8 us
    ppermute x2, waiting for transfers between devices, bring_ends(): ppermute(block_now, along_axis, [(i0, i0 ^ before) for i0 in range(num)])  44 us
    dot_general x1, matrix products, local(): gate_part = jnp.dot(normed, gate_weight, preferred_element_type=jnp.float32)  13.1 us
    dot_general x1, matrix products, local(): up_part = jnp.dot(normed, up_weight, preferred_element_type=jnp.float32)  13 us
    dot_general x1, matrix products, down_term(): return jnp.dot(row_block, down_weight, preferred_element_type=jnp.float32)  12.4 us
  transfers between devices with their start and end apart: 6, of which 6 were waited for; matrix products, arithmetic and copies ran while one was open for 4% of the time, Pallas kernels for 0%

profile of v2, /device:TPU:0, one launch (start us, length us, event | category | flops | bytes accessed | tf_op | source)
XLA Modules:
  0.0 376.7 jit_solution(4605085134377526538)
XLA Ops:
  6.5 0.0 copy-start.4
  6.5 0.0 all-gather.2.cloned.1.call-start
  6.5 0.7 all-gather.2.cloned.1.call-update
  7.3 0.0 reduce-scatter.4.cloned.1.call-start
  7.3 54.0 %all-gather.2.cloned.1.call-done = bf16[512,2048]{1,0:T(8,128)(2,1)} async-done(((bf16[64,2048]{1,0:T(8,128)(2,1)}), bf16[512,2048]{1,0:T(8,128)(2,1)}) %all-gather.2.cloned.1.call-update) | async-done | bytes 2097168 | tf_op jit(solution)/shard_map/all_gather | solution.py:34
  61.3 0.0 copy-start.2
  61.3 2.2 fusion
  63.5 5.7 %psum.7 = f32[512]{0:T(512)S(1)} all-reduce(f32[512]{0:T(512)S(1)} %fusion), channel_id=1, replica_groups=mesh['row'=4,'col'=8] {'row'}, use_global_device_ids=true, to_apply=%region_1.0 | all-reduce | flops 512 | bytes 4096 | tf_op jit(solution)/shard_map/psum | solution.py:36
  69.2 0.0 copy-done.4
  69.2 0.0 copy-done.2
  69.2 13.1 %fusion.7 = f32[512,3584]{1,0:T(8,128)} fusion(bf16[2048,3584]{1,0:T(8,128)(2,1)} %param.7, bf16[512,2048]{1,0:T(8,128)(2,1)S(1)} %copy-done.2, f32[2048]{0:T(1024)S(1)} %copy-done.4, f32[512]{0:T(512)S(1)} %add_rsqrt_fusion), kind=kOutput, calls=%fused_computation.13 | convolution fusion | flops 7520387072 | bytes 24127488 | tf_op jit(solution)/shard_map/dot_general | solution.py:38
  82.3 0.0 reduce-scatter.4.cloned.1.call-update
  82.3 0.0 reduce-scatter.6.cloned.1.call-start
  82.3 13.0 %fusion.5 = f32[512,3584]{1,0:T(8,128)} fusion(bf16[2048,3584]{1,0:T(8,128)(2,1)} %param.8, bf16[512,2048]{1,0:T(8,128)(2,1)S(1)} %copy-done.2, f32[2048]{0:T(1024)S(1)} %copy-done.4, f32[512]{0:T(512)S(1)} %add_rsqrt_fusion), kind=kOutput, calls=%fused_computation.12 | convolution fusion | flops 7520387072 | bytes 24127488 | tf_op jit(solution)/shard_map/dot_general | solution.py:39
  95.3 0.0 reduce-scatter.6.cloned.1.call-update
  95.4 0.0 reduce-scatter.8.cloned.1.call-start
  95.4 51.8 %reduce-scatter.4.cloned.1.call-done = f32[128,3584]{1,0:T(8,128)} async-done(((f32[512,3584]{1,0:T(8,128)}), f32[128,3584]{1,0:T(8,128)}) %reduce-scatter.4.cloned.1.call-update) | async-done | bytes 1835024 | tf_op jit(solution)/shard_map/reduce_scatter | solution.py:41
  147.2 0.0 copy-start
  147.2 68.5 %reduce-scatter.6.cloned.1.call-done = f32[128,3584]{1,0:T(8,128)} async-done(((f32[512,3584]{1,0:T(8,128)}), f32[128,3584]{1,0:T(8,128)}) %reduce-scatter.6.cloned.1.call-update) | async-done | bytes 1835024 | tf_op jit(solution)/shard_map/reduce_scatter | solution.py:42
  215.7 0.0 copy-start.1
  215.7 2.7 fusion.15
  218.4 0.1 collective-permute-start
  218.5 0.0 copy-done
  218.5 0.0 copy-done.1
  218.5 0.5 fusion.14
  219.0 1.9 collective-permute-done
  221.0 0.2 pad_maximum_fusion.1
  221.1 1.6 fusion.4
  222.8 0.3 collective-permute-start.1
  223.1 42.0 %collective-permute-done.1 = bf16[2,128,3584]{2,1,0:T(8,128)(2,1)} collective-permute-done((bf16[2,128,3584]{2,1,0:T(8,128)(2,1)}, bf16[2,128,3584]{2,1,0:T(8,128)(2,1)}, u32[]{:S(2)}, u32[]{:S(2)}) %collective-permute-start.1) | collective-permute-done | bytes 1835040 | tf_op jit(solution)/shard_map/ppermute | solution.py:25
  265.1 1.8 pad_maximum_fusion
  267.0 0.6 reverse_select_fusion
  267.6 12.4 %fusion.9 = f32[512,2048]{1,0:T(8,128)} fusion(bf16[512,3584]{1,0:T(8,128)(2,1)S(1)} %bitcast.15, bf16[3584,2048]{1,0:T(8,128)(2,1)} %param.9), kind=kOutput, calls=%fused_computation.16 | convolution fusion | flops 7516192768 | bytes 22544384 | tf_op jit(solution)/shard_map/dot_general | solution.py:50
  280.0 0.0 copy-start.3
  280.0 0.0 reduce-scatter.8.cloned.1.call-update
  280.0 88.4 %reduce-scatter.8.cloned.1.call-done = f32[64,2048]{1,0:T(8,128)} async-done(((f32[512,2048]{1,0:T(8,128)}), f32[64,2048]{1,0:T(8,128)}) %reduce-scatter.8.cloned.1.call-update) | async-done | bytes 524304 | tf_op jit(solution)/shard_map/reduce_scatter | solution.py:52
  368.4 0.0 copy-done.3
  368.4 1.8 add_convert_fusion
  (1 shorter events, 0.0 us)
Async XLA Ops:
  6.5 62.7 %copy-start.4 = (f32[2048]{0:T(1024)S(1)}, f32[2048]{0:T(1024)}, u32[]{:S(2)}) copy-start(f32[2048]{0:T(1024)} %param.6) | copy-start | bytes 24580
  6.5 54.8 %all-gather.2.cloned.1.call-start = ((), (), s32[]{:S(2)}) async-start(), calls=%async_computation.3 | async-start | bytes 2359296 | tf_op jit(solution)/shard_map/all_gather | solution.py:34
  7.3 139.9 %reduce-scatter.4.cloned.1.call-start = ((), (), s32[]{:S(2)}) async-start(), calls=%async_computation.4 | async-start | bytes 9175040 | tf_op jit(solution)/shard_map/reduce_scatter | solution.py:41
  61.3 7.9 %copy-start.2 = (bf16[512,2048]{1,0:T(8,128)(2,1)S(1)}, bf16[512,2048]{1,0:T(8,128)(2,1)}, u32[]{:S(2)}) copy-start(bf16[512,2048]{1,0:T(8,128)(2,1)} %all-gather.2.cloned.1.call-done) | copy-start | bytes 6291460
  82.3 133.4 %reduce-scatter.6.cloned.1.call-start = ((), (), s32[]{:S(2)}) async-start(), calls=%async_computation.5 | async-start | bytes 9175040 | tf_op jit(solution)/shard_map/reduce_scatter | solution.py:42
  95.4 273.1 %reduce-scatter.8.cloned.1.call-start = ((), (), s32[]{:S(2)}) async-start(), calls=%async_computation.6 | async-start | bytes 4718592 | tf_op jit(solution)/shard_map/reduce_scatter | solution.py:52
  147.2 71.3 %copy-start = (f32[128,3584]{1,0:T(8,128)S(1)}, f32[128,3584]{1,0:T(8,128)}, u32[]{:S(2)}) copy-start(f32[128,3584]{1,0:T(8,128)} %reduce-scatter.4.cloned.1.call-done) | copy-start | bytes 5505028
  215.7 2.8 copy-start.1
  218.4 2.5 collective-permute-start
  222.8 42.4 %collective-permute-start.1 = (bf16[2,128,3584]{2,1,0:T(8,128)(2,1)}, bf16[2,128,3584]{2,1,0:T(8,128)(2,1)}, u32[]{:S(2)}, u32[]{:S(2)}) collective-permute-start(bf16[2,128,3584]{2,1,0:T(8,128)(2,1)} %get-tuple-element.6), channel_id=1, source_target_pairs={{0,16},{8,24},{16,0},{24,8},{1,17},{9,25},{17,1},{25,9},{2,18},{10... | collective-permute-start | bytes 5505032 | tf_op jit(solution)/shard_map/ppermute | solution.py:25
  280.0 88.5 %copy-start.3 = (bf16[64,2048]{1,0:T(8,128)(2,1)S(1)}, bf16[64,2048]{1,0:T(8,128)(2,1)}, u32[]{:S(2)}) copy-start(bf16[64,2048]{1,0:T(8,128)(2,1)} %param.5) | copy-start | bytes 786436
Sparse Core Ops, SparseCore 0:
  9.5 51.7 all-gather.1
  82.4 64.7 reduce-scatter.3
  149.7 65.9 reduce-scatter.5
  280.1 88.2 reduce-scatter.7
